TPU v7x, 32 devices: a whole 2x2x4 slice. The times are simulated.
32 devices in a mesh: row: 8 (over z, y), col: 4 (over x, core).
Axes of the slice: x: 2, y: 2, z: 4, core: 2. Of those that a mesh axis runs over, the one named last changes fastest.
Arguments:
- feat_one: bfloat16 [4096, 128], P(('row', 'col')), may hold values from -16 to 16
- feat_two: bfloat16 [4096, 128], P(('col', 'row')), may hold values from -16 to 16
- value_one: bfloat16 [4096, 128], P(('row', 'col')), may hold values from -6 to 6
- value_two: bfloat16 [4096, 128], P(('col', 'row')), may hold values from -6 to 6
Outputs:
- matched_one: float32 [4096, 128], P(('row', 'col'))
- flow_one: float32 [2, 4096], P(None, ('row', 'col'))
- matched_two: float32 [4096, 128], P(('col', 'row'))
- flow_two: float32 [2, 4096], P(None, ('col', 'row'))
All inputs are finite; a program needn't handle non-finite values.
Results may differ from a plain program's by a relative error of at most 0.0011.
Values may be sent and summed in bfloat16 or wider, within the bound.
A program may use at most 128 MiB of HBM per device.

v0:
```python
import math

import jax
import jax.numpy as jnp
from jax import lax
from jax.sharding import PartitionSpec as P

GRID_W = 256


def token_coords(start, count, total):
    index = start + lax.iota(jnp.int32, count)
    across = (index % GRID_W).astype(jnp.float32) / GRID_W
    down = (index // GRID_W).astype(jnp.float32) / (total // GRID_W)
    return (across, down)


def flash_merge(first, second):
    peak_a, total_a, acc_a, across_a, down_a = first
    peak_b, total_b, acc_b, across_b, down_b = second
    peak = jnp.maximum(peak_a, peak_b)
    factor_a = jnp.exp(peak_a - peak)
    factor_b = jnp.exp(peak_b - peak)
    return (
        peak,
        total_a * factor_a + total_b * factor_b,
        acc_a * factor_a[:, None] + acc_b * factor_b[:, None],
        across_a * factor_a + across_b * factor_b,
        down_a * factor_a + down_b * factor_b,
    )


def finish(total, acc, across, down, own_across, own_down):
    matched = acc / total[:, None]
    flow = jnp.stack([across / total - own_across, down / total - own_down])
    return (matched, flow)


def body(feat_one, feat_two, value_one, value_two):
    shard = feat_one.shape[0]
    width = feat_one.shape[1]
    rows_count = lax.axis_size("row")
    cols_count = lax.axis_size("col")
    total = shard * rows_count * cols_count
    block = min(512, shard * min(rows_count, cols_count))
    src_feat, src_value = (
        lax.all_gather(feat_one, "col", axis=0, tiled=True),
        lax.all_gather(value_one, "col", axis=0, tiled=True),
    )
    tgt_feat, tgt_value = (
        lax.all_gather(feat_two, "row", axis=0, tiled=True),
        lax.all_gather(value_two, "row", axis=0, tiled=True),
    )
    n_src = src_feat.shape[0]
    n_tgt = tgt_feat.shape[0]
    row_index = lax.axis_index("row")
    col_index = lax.axis_index("col")
    src_start = row_index * n_src
    tgt_start = col_index * n_tgt
    tgt_across, tgt_down = token_coords(tgt_start, n_tgt, total)
    tgt_blocks = n_tgt // block
    across_blocks = tgt_across.reshape(tgt_blocks, block)
    down_blocks = tgt_down.reshape(tgt_blocks, block)
    value_blocks = tgt_value.reshape(tgt_blocks, block, width)
    scale = 1.0 / math.sqrt(width)

    def sweep(carry, block_index):
        start = block_index * block
        rows_feat = lax.dynamic_slice_in_dim(src_feat, start, block, 0)
        rows_value = lax.dynamic_slice_in_dim(src_value, start, block, 0)
        rows_across, rows_down = token_coords(src_start + start, block, total)
        scores = (
            lax.dot_general(
                rows_feat, tgt_feat, (((1,), (1,)), ((), ())), preferred_element_type=jnp.float32
            )
            * scale
        )
        tiled = scores.reshape(block, tgt_blocks, block)
        row_peak = jnp.max(tiled, axis=2)
        row_weight = jnp.exp(tiled - row_peak[:, :, None]).astype(jnp.bfloat16)
        weight_f = row_weight.astype(jnp.float32)
        part_total = jnp.sum(weight_f, axis=2)
        part_across = jnp.sum(weight_f * across_blocks[None], axis=2)
        part_down = jnp.sum(weight_f * down_blocks[None], axis=2)
        part_acc = jnp.einsum(
            "rkt,ktc->rkc", row_weight, value_blocks, preferred_element_type=jnp.float32
        )
        row_top = jnp.max(row_peak, axis=1)
        factor = jnp.exp(row_peak - row_top[:, None])
        row_out = (
            row_top,
            jnp.sum(factor * part_total, axis=1),
            jnp.sum(factor[:, :, None] * part_acc, axis=1),
            jnp.sum(factor * part_across, axis=1),
            jnp.sum(factor * part_down, axis=1),
        )
        col_peak = jnp.max(scores, axis=0)
        col_weight = jnp.exp(scores - col_peak[None]).astype(jnp.bfloat16)
        cweight_f = col_weight.astype(jnp.float32)
        col_acc = lax.dot_general(
            col_weight, rows_value, (((0,), (0,)), ((), ())), preferred_element_type=jnp.float32
        )
        col_part = (
            col_peak,
            jnp.sum(cweight_f, axis=0),
            col_acc,
            jnp.sum(cweight_f * rows_across[:, None], axis=0),
            jnp.sum(cweight_f * rows_down[:, None], axis=0),
        )
        return (flash_merge(carry, col_part), row_out)

    init = (
        jnp.full((n_tgt,), -jnp.inf, jnp.float32),
        jnp.zeros((n_tgt,), jnp.float32),
        jnp.zeros((n_tgt, width), jnp.float32),
        jnp.zeros((n_tgt,), jnp.float32),
        jnp.zeros((n_tgt,), jnp.float32),
    )
    col_stats, row_out = lax.scan(sweep, init, jnp.arange(n_src // block, dtype=jnp.int32))
    row_stats = (
        row_out[0].reshape(n_src),
        row_out[1].reshape(n_src),
        row_out[2].reshape(n_src, width),
        row_out[3].reshape(n_src),
        row_out[4].reshape(n_src),
    )
    one_across, one_down = token_coords(src_start + col_index * shard, shard, total)
    two_across, two_down = token_coords(tgt_start + row_index * shard, shard, total)
    row_top = lax.pmax(row_stats[0], "col")
    col_top = lax.pmax(col_stats[0], "row")
    row_factor = jnp.exp(row_stats[0] - row_top)
    col_factor = jnp.exp(col_stats[0] - col_top)
    row_total, row_acc, row_across, row_down = (
        lax.psum_scatter(row_stats[1] * row_factor, "col", scatter_dimension=0, tiled=True),
        lax.psum_scatter(
            row_stats[2] * row_factor[:, None], "col", scatter_dimension=0, tiled=True
        ),
        lax.psum_scatter(row_stats[3] * row_factor, "col", scatter_dimension=0, tiled=True),
        lax.psum_scatter(row_stats[4] * row_factor, "col", scatter_dimension=0, tiled=True),
    )
    col_total, col_acc, col_across, col_down = (
        lax.psum_scatter(col_stats[1] * col_factor, "row", scatter_dimension=0, tiled=True),
        lax.psum_scatter(
            col_stats[2] * col_factor[:, None], "row", scatter_dimension=0, tiled=True
        ),
        lax.psum_scatter(col_stats[3] * col_factor, "row", scatter_dimension=0, tiled=True),
        lax.psum_scatter(col_stats[4] * col_factor, "row", scatter_dimension=0, tiled=True),
    )
    matched_one, flow_one = finish(row_total, row_acc, row_across, row_down, one_across, one_down)
    matched_two, flow_two = finish(col_total, col_acc, col_across, col_down, two_across, two_down)
    return (matched_one, flow_one, matched_two, flow_two)


def solution(mesh):
    return jax.shard_map(
        body,
        mesh=mesh,
        in_specs=(
            P(("row", "col"), None),
            P(("col", "row"), None),
            P(("row", "col"), None),
            P(("col", "row"), None),
        ),
        out_specs=(
            P(("row", "col"), None),
            P(None, ("row", "col")),
            P(("col", "row"), None),
            P(None, ("col", "row")),
        ),
        check_vma=False,
    )
```

profile of v0, /device:TPU:0, one launch (start us, length us, event | category | flops | bytes accessed | tf_op | source)
XLA Modules:
  0.0 198.6 jit_solution(14224676328401447012)
XLA Ops:
  7.2 32.8 %all_gather.13 = bf16[1024,128]{1,0:T(8,128)(2,1)S(1)} all-gather(bf16[128,128]{1,0:T(8,128)(2,1)} %param.5), channel_id=1, replica_groups=mesh['row'=8,'col'=4] {'row'}, dimensions={0}, use_global_device_ids=true | all-gather | bytes 294912 | tf_op jit(solution)/shard_map/all_gather | solution.py:51
  40.0 5.6 %all_gather.12 = bf16[512,128]{1,0:T(8,128)(2,1)S(1)} all-gather(bf16[128,128]{1,0:T(8,128)(2,1)} %param.4), channel_id=1, replica_groups=mesh['row'=8,'col'=4] {'col'}, dimensions={0}, use_global_device_ids=true | all-gather | bytes 163840 | tf_op jit(solution)/shard_map/all_gather | solution.py:47
  45.6 1.8 fusion.27
  47.4 3.0 %reshape.135 = f32[512,2,512]{2,1,0:T(2,128)S(1)} reshape(f32[512,1024]{1,0:T(8,128)} %get-tuple-element.92) | data formatting | bytes 4194304 | tf_op jit(solution)/shard_map/while/body/eval_jaxpr/reshape | solution.py:78
  50.5 7.1 %pmax.14 = f32[512]{0:T(512)S(1)} all-reduce(f32[512]{0:T(512)S(1)} %get-tuple-element.41), channel_id=1, replica_groups=mesh['row'=8,'col'=4] {'col'}, use_global_device_ids=true, to_apply=%region_3.4 | all-reduce | flops 512 | bytes 4096 | tf_op jit(solution)/shard_map/pmax | solution.py:129
  57.6 0.6 reduce_max.30
  58.2 9.2 %fusion = (f32[512,2]{1,0:T(8,128)S(1)}, f32[512,2]{1,0:T(8,128)S(1)}, f32[512,2]{1,0:T(8,128)S(1)}, bf16[512,2,512]{2,1,0:T(2,128)(2,1)}) fusion(f32[2,512]{1,0:T(2,128)S(1)} %get-tuple-element.93, f32[2,512]{1,0:T(2,128)S(1)} %get-tuple-element.94, f32[512,2,512]{2,1,0:T(2,128)S(1)} %reshape.135, f32[512,2]{1,0:T(8,128)S(1)} %reduce_max.30), kind=kLoop, calls=%fused_computation.6 | loop fusion | flops 4191232 | bytes 3170304 | tf_op jit(solution)/shard_map/while/body/eval_jaxpr/reduce_sum | solution.py:83
  67.5 0.4 multiply_reduce_fusion.1
  68.0 31.0 %all_gather.14 = bf16[1024,128]{1,0:T(8,128)(2,1)S(1)} all-gather(bf16[128,128]{1,0:T(8,128)(2,1)S(1)} %copy-done.1), channel_id=1, replica_groups=mesh['row'=8,'col'=4] {'row'}, dimensions={0}, use_global_device_ids=true | all-gather | bytes 294912 | tf_op jit(solution)/shard_map/all_gather | solution.py:52
  99.0 1.7 fusion.7
  100.7 0.9 broadcast_multiply_fusion
  101.7 21.3 %pmax.15 = f32[1024]{0:T(1024)S(1)} all-reduce(f32[1024]{0:T(1024)S(1)} %get-tuple-element.40), channel_id=1, replica_groups=mesh['row'=8,'col'=4] {'row'}, use_global_device_ids=true, to_apply=%region_15.16 | all-reduce | flops 1024 | bytes 8192 | tf_op jit(solution)/shard_map/pmax | solution.py:130
  123.0 0.6 fusion.2
  123.6 5.4 %all_gather.15 = bf16[512,128]{1,0:T(8,128)(2,1)S(1)} all-gather(bf16[128,128]{1,0:T(8,128)(2,1)S(1)} %copy-done.2), channel_id=1, replica_groups=mesh['row'=8,'col'=4] {'col'}, dimensions={0}, use_global_device_ids=true | all-gather | bytes 163840 | tf_op jit(solution)/shard_map/all_gather | solution.py:48
  129.1 1.6 fusion.5
  130.7 0.6 dynamic-slice.6
  131.9 33.1 %all-reduce.6 = (f32[1024]{0:T(1024)S(1)}, f32[1024]{0:T(1024)S(1)}, f32[1024]{0:T(1024)S(1)}) all-reduce(f32[1024]{0:T(1024)S(1)} %get-tuple-element.87, f32[1024]{0:T(1024)S(1)} %get-tuple-element.86, f32[1024]{0:T(1024)S(1)} %get-tuple-element.77), channel_id=7, replica_groups=mesh['row'=8,'col'=4] {'row'}, use_global_device_ids=true, to_apply=%region_18.19.clone | all-reduce | flops 3072 | bytes 24576
  165.1 0.6 dynamic-slice
  166.4 5.8 %all-reduce.7 = (f32[512]{0:T(512)S(1)}, f32[512]{0:T(512)S(1)}, f32[512]{0:T(512)S(1)}) all-reduce(f32[512]{0:T(512)S(1)} %get-tuple-element.91, f32[512]{0:T(512)S(1)} %get-tuple-element.90, f32[512]{0:T(512)S(1)} %get-tuple-element.82), channel_id=3, replica_groups=mesh['row'=8,'col'=4] {'col'}, use_global_device_ids=true, to_apply=%region_7.8.clone | all-reduce | flops 1536 | bytes 12288
  172.4 0.6 pad_maximum_fusion.1
  173.0 0.6 pad_maximum_fusion
  173.6 1.6 broadcast_divide_fusion.1
  175.2 15.0 %reduce-scatter.5.cloned.1.call-done = f32[128,128]{1,0:T(8,128)} async-done(((f32[1024,128]{1,0:T(8,128)}), f32[128,128]{1,0:T(8,128)}) %reduce-scatter.5.cloned.1.call-update) | async-done | bytes 65552 | tf_op jit(solution)/shard_map/reduce_scatter | solution.py:143
  190.2 1.6 broadcast_divide_fusion
  (26 shorter events, 0.6 us)
Async XLA Ops:
  7.2 166.5 %reduce-scatter.3.cloned.1.call-start = ((), (), s32[]{:S(2)}) async-start(), calls=%async_computation.2 | async-start | bytes 327680 | tf_op jit(solution)/shard_map/reduce_scatter | solution.py:135
  58.2 9.7 %copy-start.1 = (bf16[128,128]{1,0:T(8,128)(2,1)S(1)}, bf16[128,128]{1,0:T(8,128)(2,1)}, u32[]{:S(2)}) copy-start(bf16[128,128]{1,0:T(8,128)(2,1)} %param.7) | copy-start | bytes 98308
  67.8 55.1 %copy-start = (f32[512,1024]{1,0:T(8,128)S(1)}, f32[512,1024]{1,0:T(8,128)}, u32[]{:S(2)}) copy-start(f32[512,1024]{1,0:T(8,128)} %get-tuple-element.92) | copy-start | bytes 6291460
  100.7 23.0 %copy-start.2 = (bf16[128,128]{1,0:T(8,128)(2,1)S(1)}, bf16[128,128]{1,0:T(8,128)(2,1)}, u32[]{:S(2)}) copy-start(bf16[128,128]{1,0:T(8,128)(2,1)} %param.6) | copy-start | bytes 98308
  101.6 88.6 %reduce-scatter.5.cloned.1.call-start = ((), (), s32[]{:S(2)}) async-start(), calls=%async_computation.3 | async-start | bytes 589824 | tf_op jit(solution)/shard_map/reduce_scatter | solution.py:143
  123.0 7.7 %copy-start.4 = (u32[32]{0:T(128)S(1)}, u32[32]{0:T(128)}, u32[]{:S(2)}) copy-start(u32[32]{0:T(128)} %constant.158) | copy-start | bytes 388
  123.0 42.2 %copy-start.3 = (u32[32]{0:T(128)S(1)}, u32[32]{0:T(128)}, u32[]{:S(2)}) copy-start(u32[32]{0:T(128)} %constant.146) | copy-start | bytes 388
Sparse Core Ops, SparseCore 0:
  101.7 19.9 reduce-scatter.2
  130.8 59.3 reduce-scatter.4
where the time goes:
time: 199 us
  blocking collectives  142 us (71%)
  other arithmetic  16.4 us (8%)
  between operations  15.5 us (8%)
  waiting for transfers between devices  15 us (8%)
  matrix products  5.05 us (3%)
  local copies, waits for them, and re-layouts  4.34 us (2%)
    unnamed x2, blocking collectives  39 us
    all_gather x1, blocking collectives, body(): lax.all_gather(feat_two, 'row', axis=0, tiled=True)  32.8 us
    all_gather x1, blocking collectives, body(): lax.all_gather(value_two, 'row', axis=0, tiled=True)  31 us
    pmax x1, blocking collectives, body(): col_top = lax.pmax(col_stats[0], 'row')  21.3 us
    reduce_scatter x1, waiting for transfers between devices, body(): lax.psum_scatter(col_stats[2] * col_factor[:, None], 'row', scatter_dimen...  15 us
    reduce_sum x1, other arithmetic, sweep(): part_across = jnp.sum(weight_f * across_blocks[None], axis=2)  9.23 us
    pmax x1, blocking collectives, body(): row_top = lax.pmax(row_stats[0], 'col')  7.1 us
    all_gather x1, blocking collectives, body(): lax.all_gather(feat_one, 'col', axis=0, tiled=True)  5.61 us
  transfers between devices with their start and end apart: 2, of which 1 were waited for; matrix products, arithmetic and copies ran while one was open for 3% of the time, Pallas kernels for 0%

commit v1 on v0

v1 whole, which is shorter than its diff:
```python
import functools
import math

import jax
import jax.numpy as jnp
from jax import lax
from jax.experimental import pallas as pl
from jax.experimental.pallas import tpu as pltpu
from jax.sharding import PartitionSpec as P

GRID_W = 256
EXTRA = 16
STATS = 8
MESH = pl.DeviceIdType.MESH


def split_axes(rows, cols):
    cores = 2 if cols % 2 == 0 else 1
    outer = cols // cores
    low = min(
        (n for n in range(1, rows + 1) if rows % n == 0),
        key=lambda n: abs(n * outer - rows // n),
    )
    return rows // low, low, outer, cores


def coords(block, shard, total, shape):
    index = block * shard + lax.broadcasted_iota(jnp.int32, shape, len(shape) - 1)
    across = lax.rem(index, GRID_W).astype(jnp.float32) / GRID_W
    down = lax.div(index, GRID_W).astype(jnp.float32) / (total // GRID_W)
    return across, down


def values_under(block, value, shard, total):
    across, down = coords(block, shard, total, (EXTRA, shard))
    line = lax.broadcasted_iota(jnp.int32, (EXTRA, shard), 0)
    extra = jnp.where(line == 0, 1.0, jnp.where(line == 1, across, jnp.where(line == 2, down, 0.0)))
    turned = jnp.transpose(value.astype(jnp.float32))
    return jnp.concatenate([turned, extra], axis=0).astype(jnp.bfloat16)


def attend(keys, queries, under, width, rate):
    scores = lax.dot_general(
        keys, queries, (((1,), (1,)), ((), ())), preferred_element_type=jnp.float32
    )
    peak = jnp.max(scores, axis=0, keepdims=True)
    weight = jnp.exp2((scores - peak) * rate).astype(jnp.bfloat16)
    sums = jnp.dot(under, weight, preferred_element_type=jnp.float32)
    stats = sums[width : width + STATS]
    line = lax.broadcasted_iota(jnp.int32, stats.shape, 0)
    stats = jnp.where(line == 3, peak, stats)
    return jnp.concatenate([sums[:width], stats], axis=0)


def merge(packets, width, rate):
    peaks = [p[width + 3 : width + 4] for p in packets]
    top = functools.reduce(jnp.maximum, peaks)
    total = None
    for packet, peak in zip(packets, peaks):
        term = packet * jnp.exp2((peak - top) * rate)
        total = term if total is None else total + term
    return total, top


def kernel(
    dims, total, rate,
    feat_one, feat_two, value_one, value_two,
    matched_one, flow_one, matched_two, flow_two,
    f1, v1, f2, v2, under1, under2, part1, pair1, send1, got1, part2, got2,
    load_sem, f1s, f1r, v1s, v1r, g1s, g1r, w1s, w1r, f2s, f2r, v2s, v2r,
    p2s, p2r, q1s, q1r, p1s, p1r,
):
    high, low, outer, cores = dims
    rows, cols = high * low, outer * cores
    plane = low * outer
    shard, width = feat_one.shape
    row, col = lax.axis_index("row"), lax.axis_index("col")
    h, l = row // low, row % low
    x, k = col // cores, col % cores
    p = l * outer + x

    def in_plane(step):
        q = (p + step + plane) % plane
        return (h * low + q // outer, (q % outer) * cores + k)

    def in_line(step):
        return (((h + step + high) % high) * low + l, col)

    partner = (row, x * cores + (cores - 1 - k))

    def block_one(slot):
        q = (p - slot % plane + plane) % plane
        core = k if slot < plane else cores - 1 - k
        return (h * low + q // outer) * cols + (q % outer) * cores + core

    def block_two(slot):
        return col * rows + ((h - slot + high) % high) * low + l

    def span(slot):
        return pl.ds(slot * shard, shard)

    loads = [
        pltpu.make_async_copy(src, dst.at[span(0)], load_sem.at[n])
        for n, (src, dst) in enumerate(
            ((feat_two, f2), (feat_one, f1), (value_one, v1), (value_two, v2))
        )
    ]
    for load in loads:
        load.start()

    peers = [in_plane(d) for d in range(1, plane)] + [in_line(e) for e in range(1, high)]
    if cores == 2:
        peers.append(partner)
    barrier = pltpu.get_barrier_semaphore()
    for peer in peers:
        pl.semaphore_signal(barrier, inc=1, device_id=peer, device_id_type=MESH)
    pl.semaphore_wait(barrier, len(peers))

    started = []

    def send(src, dst, ssem, rsem, peer):
        copy = pltpu.make_async_remote_copy(
            src_ref=src, dst_ref=dst, send_sem=ssem, recv_sem=rsem,
            device_id=peer, device_id_type=MESH,
        )
        copy.start()
        started.append(copy)
        return copy

    def gather(buf, ssem, rsem, count, peer_of):
        return [None] + [
            send(buf.at[span(0)], buf.at[span(s)], ssem.at[s], rsem.at[s], peer_of(s))
            for s in range(1, count)
        ]

    def forward(buf, slot, ssem, rsem):
        return send(
            buf.at[span(slot)], buf.at[span(plane + slot)], ssem.at[slot], rsem.at[slot], partner
        )

    loads[0].wait()
    f2c = gather(f2, f2s, f2r, high, in_line)
    loads[1].wait()
    f1c = gather(f1, f1s, f1r, plane, in_plane)
    loads[2].wait()
    v1c = gather(v1, v1s, v1r, plane, in_plane)
    loads[3].wait()
    v2c = gather(v2, v2s, v2r, high, in_line)
    f1f, v1f = [], []

    def keep_one(slot):
        under1[:, span(slot)] = values_under(block_one(slot), v1[span(slot), :], shard, total)

    for s in range(plane):
        if s:
            f1c[s].wait_recv()
        if cores == 2:
            f1f.append(forward(f1, s, g1s, g1r))
        if s:
            v1c[s].wait_recv()
        if cores == 2:
            v1f.append(forward(v1, s, w1s, w1r))
        keep_one(s)
    if cores == 2:
        for s in range(plane):
            f1f[s].wait_recv()
            v1f[s].wait_recv()
            keep_one(plane + s)

    p2c = []
    for s in range(high):
        if s:
            f2c[s].wait_recv()
        part2[s] = attend(f1[...], f2[span(s), :], under1[...], width, rate)
        if s:
            p2c.append(send(part2.at[s], got2.at[s], p2s.at[s], p2r.at[s], in_line(-s)))
    for s in range(high):
        if s:
            v2c[s].wait_recv()
        under2[:, span(s)] = values_under(block_two(s), v2[span(s), :], shard, total)

    step = 2 if plane % 2 == 0 else 1
    q1c, p1c = [], []
    for kind in reversed(range(cores)):
        for s in range(0, plane, step):
            first = kind * plane + s
            out = attend(
                f2[...], f1[pl.ds(first * shard, step * shard), :], under2[...], width, rate
            )
            for n in range(step):
                part1[first + n] = out[:, n * shard : (n + 1) * shard]
                if kind == 1:
                    q1c.append(
                        send(part1.at[first + n], pair1.at[s + n], q1s.at[s + n], q1r.at[s + n], partner)
                    )
    line = lax.broadcasted_iota(jnp.int32, (width + STATS, shard), 0)
    for s in reversed(range(plane)):
        if cores == 2:
            q1c[s].wait_recv()
            sums, top = merge([part1[s], pair1[s]], width, rate)
            send1[s] = jnp.where(line == width + 3, top, sums)
        else:
            send1[s] = part1[s]
        if s:
            p1c.append(send(send1.at[s], got1.at[s], p1s.at[s], p1r.at[s], in_plane(-s)))

    def finish(packets, block, matched, flow):
        sums, _ = merge(packets, width, rate)
        inverse = 1.0 / sums[width : width + 1]
        matched[...] = jnp.transpose(sums[:width] * inverse)
        across, down = coords(block, shard, total, (1, shard))
        flow[0:1, :] = sums[width + 1 : width + 2] * inverse - across
        flow[1:2, :] = sums[width + 2 : width + 3] * inverse - down

    for copy in p2c:
        copy.wait_recv()
    finish([part2[0]] + [got2[s] for s in range(1, high)], block_two(0), matched_two, flow_two)
    for copy in p1c:
        copy.wait_recv()
    finish([send1[0]] + [got1[s] for s in range(1, plane)], block_one(0), matched_one, flow_one)
    for copy in started:
        copy.wait_send()


def body(feat_one, feat_two, value_one, value_two):
    shard, width = feat_one.shape
    rows, cols = lax.axis_size("row"), lax.axis_size("col")
    dims = split_axes(rows, cols)
    high, low, outer, cores = dims
    plane = low * outer
    total = shard * rows * cols
    rate = math.log2(math.e) / math.sqrt(width)
    bf16, f32 = jnp.bfloat16, jnp.float32
    n1, n2 = plane * cores * shard, high * shard
    packet = (width + STATS, shard)
    vmem = pltpu.VMEM
    dma = pltpu.SemaphoreType.DMA
    return pl.pallas_call(
        functools.partial(kernel, dims, total, rate),
        out_shape=(
            jax.ShapeDtypeStruct((shard, width), f32),
            jax.ShapeDtypeStruct((2, shard), f32),
            jax.ShapeDtypeStruct((shard, width), f32),
            jax.ShapeDtypeStruct((2, shard), f32),
        ),
        in_specs=[pl.BlockSpec(memory_space=pl.ANY)] * 4,
        out_specs=[pl.BlockSpec(memory_space=pltpu.VMEM)] * 4,
        scratch_shapes=[
            vmem((n1, width), bf16),
            vmem((n1, width), bf16),
            vmem((n2, width), bf16),
            vmem((n2, width), bf16),
            vmem((width + EXTRA, n1), bf16),
            vmem((width + EXTRA, n2), bf16),
            vmem((plane * cores,) + packet, f32),
            vmem((plane,) + packet, f32),
            vmem((plane,) + packet, f32),
            vmem((plane,) + packet, f32),
            vmem((high,) + packet, f32),
            vmem((high,) + packet, f32),
            dma((4,)),
        ]
        + [dma((plane,))] * 8
        + [dma((high,))] * 6
        + [dma((plane,))] * 4,
        compiler_params=pltpu.CompilerParams(collective_id=0, has_side_effects=True),
        name="match",
    )(feat_one, feat_two, value_one, value_two)


def solution(mesh):
    return jax.shard_map(
        body,
        mesh=mesh,
        in_specs=(
            P(("row", "col"), None),
            P(("col", "row"), None),
            P(("row", "col"), None),
            P(("col", "row"), None),
        ),
        out_specs=(
            P(("row", "col"), None),
            P(None, ("row", "col")),
            P(("col", "row"), None),
            P(None, ("col", "row")),
        ),
        check_vma=False,
    )
```

time: 199 us -> 27 us (0.14)
  blocking collectives: 142 us -> 0 us
  Pallas kernels: 0 us -> 22.8 us
  other arithmetic: 16.4 us -> 0 us
  waiting for transfers between devices: 15 us -> 0 us
  between operations: 15.5 us -> 0.66 us
  matrix products: 5.05 us -> 0 us
    all_gather x4 -> x0, blocking collectives: 74.8 us -> none  [the longest x1 32.8 us: body(): lax.all_gather(feat_two, 'row', axis=0, tiled=True)]
    unnamed x2 -> x0, blocking collectives: 39 us -> none
    pmax x2 -> x0, blocking collectives: 28.4 us -> none  [the longest x1 21.3 us: body(): col_top = lax.pmax(col_stats[0], 'row')]
    pallas_call x0 -> x1, Pallas kernels: none -> 22.8 us  [body(): pl.pallas_call(functools.partial(kernel, dims, total, rate), out_shape=(j...]
    reduce_scatter x2 -> x0, waiting for transfers between devices: 15 us -> none  [the longest x1 15 us: body(): lax.psum_scatter(col_stats[2] * col_factor[:, None], 'row', scatter_dimen...]
    reduce_sum x3 -> x0, other arithmetic: 10.2 us -> none  [the longest x1 9.23 us: sweep(): part_across = jnp.sum(weight_f * across_blocks[None], axis=2)]
    dot_general x3 -> x0, matrix products: 5.05 us -> none  [the longest x1 1.79 us: sweep(): lax.dot_general(rows_feat, tgt_feat, (((1,), (1,)), ((), ())), preferred_...]
    div x4 -> x0, other arithmetic: 3.16 us -> none  [the longest x2 3.12 us: finish(): matched = acc / total[:, None]]
  transfers between devices with their start and end apart: 2 -> 0, of which waited for: 1 -> 0; matrix products, arithmetic and copies ran while one was open for 3% -> 0% of each run, Pallas kernels for 0% -> 0%
where the time goes in v1:
time: 27 us; the launch traced here: 26.8 us
  Pallas kernels  22.8 us (84%)
  local copies, waits for them, and re-layouts  3.27 us (12%)
  between operations  0.66 us (2%)
    pallas_call x1, Pallas kernels, body(): pl.pallas_call(functools.partial(kernel, dims, total, rate), out_shape=(j...  22.8 us
    unnamed x10, local copies, waits for them, and re-layouts  3.27 us

profile of v1, /device:TPU:0, one launch (start us, length us, event | category | flops | bytes accessed | tf_op | source)
XLA Modules:
  0.0 26.8 jit_solution(3991761029648305837)
XLA Ops:
  0.6 22.8 %match.1 = (f32[128,128]{1,0:T(8,128)}, f32[2,128]{1,0:T(2,128)}, f32[128,128]{1,0:T(8,128)}, f32[2,128]{1,0:T(2,128)}) custom-call(bf16[128,128]{1,0:T(8,128)(2,1)} %feat_one.1, bf16[128,128]{1,0:T(8,128)(2,1)} %feat_two.1, bf16[128,128]{1,0:T(8,128)(2,1)} %value_one.1, bf16[128,128]{1,0:T(8,128)(2,1)} %value_two.1), custom_call_target="tpu_custom_call" | custom-call | tf_op jit(solution)/shard_map/match/pallas_call | solution.py:238
  23.5 0.0 copy-start.2
  23.5 0.0 copy-start
  23.5 1.5 %copy.12 = f32[128,128]{1,0:T(8,128)} copy(f32[128,128]{1,0:T(8,128)} %get-tuple-element.8) | data formatting | bytes 131072
  25.0 0.0 copy-done.2
  25.0 0.6 %copy.13 = f32[2,128]{1,0:T(2,128)} copy(f32[2,128]{1,0:T(2,128)S(1)} %copy-done.2) | data formatting | bytes 2048
  25.6 0.0 copy-done
  25.6 0.0 copy-start.1
  25.6 0.6 %copy.14 = f32[128,128]{1,0:T(8,128)} copy(f32[128,128]{1,0:T(8,128)S(1)} %copy-done) | data formatting | bytes 131072
  26.2 0.0 copy-done.1
  26.2 0.6 %copy.15 = f32[2,128]{1,0:T(2,128)} copy(f32[2,128]{1,0:T(2,128)S(1)} %copy-done.1) | data formatting | bytes 2048
Async XLA Ops:
  23.5 1.5 %copy-start.2 = (f32[2,128]{1,0:T(2,128)S(1)}, f32[2,128]{1,0:T(2,128)}, u32[]{:S(2)}) copy-start(f32[2,128]{1,0:T(2,128)} %get-tuple-element.9) | copy-start | bytes 3076
  23.5 2.1 %copy-start = (f32[128,128]{1,0:T(8,128)S(1)}, f32[128,128]{1,0:T(8,128)}, u32[]{:S(2)}) copy-start(f32[128,128]{1,0:T(8,128)} %get-tuple-element.10) | copy-start | bytes 196612
  25.6 0.6 %copy-start.1 = (f32[2,128]{1,0:T(2,128)S(1)}, f32[2,128]{1,0:T(2,128)}, u32[]{:S(2)}) copy-start(f32[2,128]{1,0:T(2,128)} %get-tuple-element.11) | copy-start | bytes 3076

commit v2 on v1

v2 whole, which is shorter than its diff:
```python
import functools
import math

import jax
import jax.numpy as jnp
from jax import lax
from jax.experimental import pallas as pl
from jax.experimental.pallas import tpu as pltpu
from jax.sharding import PartitionSpec as P

GRID_W = 256
EXTRA = 16
STATS = 8
SPAN = 240.0
MESH = pl.DeviceIdType.MESH


def split_axes(rows, cols):
    cores = 2 if cols % 2 == 0 else 1
    outer = cols // cores
    low = min(
        (n for n in range(1, rows + 1) if rows % n == 0),
        key=lambda n: abs(n * outer - rows // n),
    )
    return rows // low, low, outer, cores


def coords(block, shard, total, shape):
    index = block * shard + lax.broadcasted_iota(jnp.int32, shape, len(shape) - 1)
    across = lax.rem(index, GRID_W).astype(jnp.float32) / GRID_W
    down = lax.div(index, GRID_W).astype(jnp.float32) / (total // GRID_W)
    return across, down


def values_under(block, value, shard, total):
    across, down = coords(block, shard, total, (EXTRA, shard))
    line = lax.broadcasted_iota(jnp.int32, (EXTRA, shard), 0)
    extra = jnp.where(line == 0, 1.0, jnp.where(line == 1, across, jnp.where(line == 2, down, 0.0)))
    turned = jnp.transpose(value.astype(jnp.float32))
    return jnp.concatenate([turned, extra], axis=0).astype(jnp.bfloat16)


def weigh(keys, queries, rate):
    scores = lax.dot_general(
        keys, queries, (((1,), (1,)), ((), ())), preferred_element_type=jnp.float32
    )
    peak = jnp.max(scores, axis=0, keepdims=True)
    return jnp.exp2((scores - peak) * rate).astype(jnp.bfloat16), peak


def collect(under, weight, peak, width):
    sums = jnp.dot(under, weight, preferred_element_type=jnp.float32)
    acc, stats = sums[:width], sums[width : width + STATS]
    line = lax.broadcasted_iota(jnp.int32, stats.shape, 0)
    return acc, jnp.where(line == 3, peak, stats)


def encode(acc, stats):
    size = jnp.abs(acc)
    big = jnp.maximum(jnp.max(size, axis=0, keepdims=True), 1e-30)
    code = jnp.exp2(size * (SPAN / big) - SPAN / 2)
    line = lax.broadcasted_iota(jnp.int32, stats.shape, 0)
    return jnp.where(acc < 0, -code, code).astype(jnp.bfloat16), jnp.where(line == 4, big, stats)


def decode(code, stats):
    code = code.astype(jnp.float32)
    size = jnp.log(jnp.abs(code)) * (1.0 / (SPAN * math.log(2.0))) + 0.5
    return jnp.where(code < 0, -size, size) * stats[4:5]


def merge(packets, rate):
    top = functools.reduce(jnp.maximum, [stats[3:4] for _, stats in packets])
    acc_all, stats_all = 0.0, 0.0
    for acc, stats in packets:
        factor = jnp.exp2((stats[3:4] - top) * rate)
        acc_all += acc * factor
        stats_all += stats * factor
    return acc_all, stats_all


def kernel(
    dims, total, rate,
    feat_one, feat_two, value_one, value_two,
    out_one, out_two,
    f1, v1, f2, v2, under1, under2, weight1, peak1, own1, own2,
    code1, stat1, got_code1, got_stat1, code2, stat2, got_code2, got_stat2,
    load_sem, f1s, f1r, v1s, v1r, g1s, g1r, w1s, w1r, f2s, f2r, v2s, v2r,
    c2s, c2r, t2s, t2r, c1s, c1r, t1s, t1r,
):
    high, low, outer, cores = dims
    rows, cols = high * low, outer * cores
    plane = low * outer
    shard, width = feat_one.shape
    row, col = lax.axis_index("row"), lax.axis_index("col")
    h, l = row // low, row % low
    x, k = col // cores, col % cores
    p = l * outer + x

    def in_plane(step, kind=0):
        q = (p + step + plane) % plane
        return (h * low + q // outer, (q % outer) * cores + (cores - 1 - k if kind else k))

    def in_line(step):
        return (((h + step + high) % high) * low + l, col)

    partner = in_plane(0, 1)

    def block_one(slot):
        q = (p - slot % plane + plane) % plane
        core = k if slot < plane else cores - 1 - k
        return (h * low + q // outer) * cols + (q % outer) * cores + core

    def block_two(slot):
        return col * rows + ((h - slot + high) % high) * low + l

    def span(slot):
        return pl.ds(slot * shard, shard)

    loads = [
        pltpu.make_async_copy(src, dst.at[span(0)], load_sem.at[n])
        for n, (src, dst) in enumerate(
            ((feat_two, f2), (feat_one, f1), (value_one, v1), (value_two, v2))
        )
    ]
    for load in loads:
        load.start()

    peers = [in_line(e) for e in range(1, high)]
    peers += [in_plane(d, kind) for kind in range(cores) for d in range(plane) if d or kind]
    barrier = pltpu.get_barrier_semaphore()
    for peer in peers:
        pl.semaphore_signal(barrier, inc=1, device_id=peer, device_id_type=MESH)
    pl.semaphore_wait(barrier, len(peers))

    started = []

    def send(src, dst, ssem, rsem, peer):
        copy = pltpu.make_async_remote_copy(
            src_ref=src, dst_ref=dst, send_sem=ssem, recv_sem=rsem,
            device_id=peer, device_id_type=MESH,
        )
        copy.start()
        started.append(copy)
        return copy

    def gather(buf, ssem, rsem, count, peer_of):
        return [None] + [
            send(buf.at[span(0)], buf.at[span(s)], ssem.at[s], rsem.at[s], peer_of(s))
            for s in range(1, count)
        ]

    def forward(buf, slot, ssem, rsem):
        return send(
            buf.at[span(slot)], buf.at[span(plane + slot)], ssem.at[slot], rsem.at[slot], partner
        )

    loads[0].wait()
    f2c = gather(f2, f2s, f2r, high, in_line)
    loads[1].wait()
    f1c = gather(f1, f1s, f1r, plane, in_plane)
    loads[2].wait()
    v1c = gather(v1, v1s, v1r, plane, in_plane)
    loads[3].wait()
    v2c = gather(v2, v2s, v2r, high, in_line)
    f1f, v1f = [], []

    def keep_one(slot):
        under1[:, span(slot)] = values_under(block_one(slot), v1[span(slot), :], shard, total)

    for s in range(plane):
        if s:
            f1c[s].wait_recv()
        if cores == 2:
            f1f.append(forward(f1, s, g1s, g1r))
    for s in range(plane):
        if s:
            v1c[s].wait_recv()
        if cores == 2:
            v1f.append(forward(v1, s, w1s, w1r))
        keep_one(s)
    if cores == 2:
        for s in range(plane):
            f1f[s].wait_recv()
            v1f[s].wait_recv()
            keep_one(plane + s)

    c2c, c1c = [], []
    for s in range(high):
        if s:
            f2c[s].wait_recv()
        acc, stats = collect(under1[...], *weigh(f1[...], f2[span(s), :], rate), width)
        if s:
            code2[s], stat2[s] = encode(acc, stats)
            c2c.append(send(code2.at[s], got_code2.at[s], c2s.at[s], c2r.at[s], in_line(-s)))
            c2c.append(send(stat2.at[s], got_stat2.at[s], t2s.at[s], t2r.at[s], in_line(-s)))
        else:
            own2[:width], own2[width:] = acc, stats

    step = 2 if plane % 2 == 0 else 1
    for s in range(0, plane * cores, step):
        at = pl.ds(s * shard, step * shard)
        weight1[:, at], peak1[:, at] = weigh(f2[...], f1[at, :], rate)
    for s in range(high):
        if s:
            v2c[s].wait_recv()
        under2[:, span(s)] = values_under(block_two(s), v2[span(s), :], shard, total)
    for s in reversed(range(0, plane * cores, step)):
        at = pl.ds(s * shard, step * shard)
        accs, statss = collect(under2[...], weight1[:, at], peak1[:, at], width)
        for n in range(step):
            slot, lanes = s + n, slice(n * shard, (n + 1) * shard)
            acc, stats = accs[:, lanes], statss[:, lanes]
            if slot:
                owner = in_plane(-(slot % plane), slot // plane)
                code1[slot], stat1[slot] = encode(acc, stats)
                c1c.append(
                    send(code1.at[slot], got_code1.at[slot], c1s.at[slot], c1r.at[slot], owner)
                )
                c1c.append(
                    send(stat1.at[slot], got_stat1.at[slot], t1s.at[slot], t1r.at[slot], owner)
                )
            else:
                own1[:width], own1[width:] = acc, stats

    def finish(own, codes, stats, count, block, out):
        packets = [(own[:width], own[width:])]
        packets += [(decode(codes[n], stats[n]), stats[n]) for n in range(1, count)]
        acc, sums = merge(packets, rate)
        inverse = 1.0 / sums[0:1]
        out[:width] = acc * inverse
        across, down = coords(block, shard, total, (STATS, shard))
        line = lax.broadcasted_iota(jnp.int32, sums.shape, 0)
        out[width:] = sums * inverse - jnp.where(line == 1, across, down)

    for copy in c2c:
        copy.wait_recv()
    finish(own2, got_code2, got_stat2, high, block_two(0), out_two)
    for copy in c1c:
        copy.wait_recv()
    finish(own1, got_code1, got_stat1, plane * cores, block_one(0), out_one)
    for copy in started:
        copy.wait_send()


def place(one, two, matched_one, flow_one, matched_two, flow_two):
    width = matched_one.shape[1]
    for packet, matched, flow in ((one, matched_one, flow_one), (two, matched_two, flow_two)):
        matched[...] = jnp.transpose(packet[:width])
        flow[...] = packet[width + 1 : width + 3]


def body(feat_one, feat_two, value_one, value_two):
    shard, width = feat_one.shape
    rows, cols = lax.axis_size("row"), lax.axis_size("col")
    dims = split_axes(rows, cols)
    high, low, outer, cores = dims
    plane = low * outer
    total = shard * rows * cols
    rate = math.log2(math.e) / math.sqrt(width)
    bf16, f32 = jnp.bfloat16, jnp.float32
    n1, n2 = plane * cores * shard, high * shard
    packet = (width + STATS, shard)
    vmem = pltpu.VMEM
    dma = pltpu.SemaphoreType.DMA
    one, two = pl.pallas_call(
        functools.partial(kernel, dims, total, rate),
        out_shape=(jax.ShapeDtypeStruct(packet, f32),) * 2,
        in_specs=[pl.BlockSpec(memory_space=pltpu.HBM)] * 4,
        out_specs=[pl.BlockSpec(memory_space=pltpu.VMEM)] * 2,
        scratch_shapes=[
            vmem((n1, width), bf16),
            vmem((n1, width), bf16),
            vmem((n2, width), bf16),
            vmem((n2, width), bf16),
            vmem((width + EXTRA, n1), bf16),
            vmem((width + EXTRA, n2), bf16),
            vmem((n2, n1), bf16),
            vmem((1, n1), f32),
            vmem(packet, f32),
            vmem(packet, f32),
            vmem((plane * cores, width, shard), bf16),
            vmem((plane * cores, STATS, shard), f32),
            vmem((plane * cores, width, shard), bf16),
            vmem((plane * cores, STATS, shard), f32),
            vmem((high, width, shard), bf16),
            vmem((high, STATS, shard), f32),
            vmem((high, width, shard), bf16),
            vmem((high, STATS, shard), f32),
            dma((4,)),
        ]
        + [dma((plane,))] * 8
        + [dma((high,))] * 8
        + [dma((plane * cores,))] * 4,
        compiler_params=pltpu.CompilerParams(
            collective_id=0,
            has_side_effects=True,
        ),
        name="match",
    )(feat_one, feat_two, value_one, value_two)
    return pl.pallas_call(
        place,
        out_shape=(
            jax.ShapeDtypeStruct((shard, width), f32),
            jax.ShapeDtypeStruct((2, shard), f32),
            jax.ShapeDtypeStruct((shard, width), f32),
            jax.ShapeDtypeStruct((2, shard), f32),
        ),
        in_specs=[pl.BlockSpec(memory_space=pltpu.VMEM)] * 2,
        out_specs=[pl.BlockSpec(memory_space=pltpu.VMEM)] * 4,
        name="place",
    )(one, two)


def solution(mesh):
    return jax.shard_map(
        body,
        mesh=mesh,
        in_specs=(
            P(("row", "col"), None),
            P(("col", "row"), None),
            P(("row", "col"), None),
            P(("col", "row"), None),
        ),
        out_specs=(
            P(("row", "col"), None),
            P(None, ("row", "col")),
            P(("col", "row"), None),
            P(None, ("col", "row")),
        ),
        check_vma=False,
    )
```

time: 27 us -> 24.5 us (0.907)
  local copies, waits for them, and re-layouts: 3.27 us -> 0 us
  Pallas kernels: 22.8 us -> 23.6 us
    unnamed x10 -> x0, local copies, waits for them, and re-layouts: 3.27 us -> none
    pallas_call x0 -> x1, Pallas kernels: none -> 1.67 us  [body(): pl.pallas_call(place, out_shape=(jax.ShapeDtypeStruct((shard, width), f32...]
    pallas_call x1, Pallas kernels: 22.8 us -> 22 us  [body(): pl.pallas_call(functools.partial(kernel, dims, total, rate), out_shape=(j...]
where the time goes in v2:
time: 24.5 us; the launch traced here: 24.3 us
  Pallas kernels  23.6 us (96%)
  between operations  0.64 us (3%)
    pallas_call x1, Pallas kernels, body(): pl.pallas_call(functools.partial(kernel, dims, total, rate), out_shape=(j...  22 us
    pallas_call x1, Pallas kernels, body(): pl.pallas_call(place, out_shape=(jax.ShapeDtypeStruct((shard, width), f32...  1.67 us

profile of v2, /device:TPU:0, one launch (start us, length us, event | category | flops | bytes accessed | tf_op | source)
XLA Modules:
  0.0 24.3 jit_solution(4564316565685439633)
XLA Ops:
  0.6 22.0 %match.1 = (f32[136,128]{1,0:T(8,128)}, f32[136,128]{1,0:T(8,128)}) custom-call(bf16[128,128]{1,0:T(8,128)(2,1)} %feat_one.1, bf16[128,128]{1,0:T(8,128)(2,1)} %feat_two.1, bf16[128,128]{1,0:T(8,128)(2,1)} %value_one.1, bf16[128,128]{1,0:T(8,128)(2,1)} %value_two.1), custom_call_target="tpu_custom_call" | custom-call | tf_op jit(solution)/shard_map/match/pallas_call | solution.py:266
  22.6 1.7 %place.1 = (f32[128,128]{1,0:T(8,128)}, f32[2,128]{1,0:T(2,128)}, f32[128,128]{1,0:T(8,128)}, f32[2,128]{1,0:T(2,128)}) custom-call(f32[136,128]{1,0:T(8,128)} %get-tuple-element.6.one, f32[136,128]{1,0:T(8,128)} %get-tuple-element.7.two), custom_call_target="tpu_custom_call" | custom-call | tf_op jit(solution)/shard_map/place/pallas_call | solution.py:301

commit v3 on v2

--- a/solution.py
+++ b/solution.py
@@ -83,7 +83,7 @@
     dims, total, rate,
     feat_one, feat_two, value_one, value_two,
     out_one, out_two,
-    f1, v1, f2, v2, under1, under2, weight1, peak1, own1, own2,
+    f1, v1, f2, v2, under1, under2, weight1, peak1, weight2, peak2, own1, own2,
     code1, stat1, got_code1, got_stat1, code2, stat2, got_code2, got_stat2,
     load_sem, f1s, f1r, v1s, v1r, g1s, g1r, w1s, w1r, f2s, f2r, v2s, v2r,
     c2s, c2r, t2s, t2r, c1s, c1r, t1s, t1r,
@@ -179,33 +179,45 @@
         if cores == 2:
             v1f.append(forward(v1, s, w1s, w1r))
         keep_one(s)
-    if cores == 2:
-        for s in range(plane):
-            f1f[s].wait_recv()
-            v1f[s].wait_recv()
-            keep_one(plane + s)
-
-    c2c, c1c = [], []
+    for copy in f1f:
+        copy.wait_recv()
+
+    c2c, c1c = {}, {}
+    step = 2 if plane % 2 == 0 else 1
+    wide = 2 if high % 2 == 0 else 1
     for s in range(high):
         if s:
             f2c[s].wait_recv()
-        acc, stats = collect(under1[...], *weigh(f1[...], f2[span(s), :], rate), width)
-        if s:
-            code2[s], stat2[s] = encode(acc, stats)
-            c2c.append(send(code2.at[s], got_code2.at[s], c2s.at[s], c2r.at[s], in_line(-s)))
-            c2c.append(send(stat2.at[s], got_stat2.at[s], t2s.at[s], t2r.at[s], in_line(-s)))
-        else:
-            own2[:width], own2[width:] = acc, stats
-
-    step = 2 if plane % 2 == 0 else 1
-    for s in range(0, plane * cores, step):
+        if s % wide == wide - 1:
+            at = pl.ds((s - wide + 1) * shard, wide * shard)
+            weight2[:, at], peak2[:, at] = weigh(f1[...], f2[at, :], rate)
+    for s, copy in enumerate(v1f):
+        copy.wait_recv()
+        keep_one(plane + s)
+    for s in reversed(range(0, high, wide)):
+        at = pl.ds(s * shard, wide * shard)
+        accs, statss = collect(under1[...], weight2[:, at], peak2[:, at], width)
+        for n in range(wide):
+            slot, lanes = s + n, slice(n * shard, (n + 1) * shard)
+            acc, stats = accs[:, lanes], statss[:, lanes]
+            if slot:
+                back = in_line(-slot)
+                code2[slot], stat2[slot] = encode(acc, stats)
+                c2c[slot] = (
+                    send(code2.at[slot], got_code2.at[slot], c2s.at[slot], c2r.at[slot], back),
+                    send(stat2.at[slot], got_stat2.at[slot], t2s.at[slot], t2r.at[slot], back),
+                )
+            else:
+                own2[:width], own2[width:] = acc, stats
+    for s in reversed(range(0, plane * cores, step)):
         at = pl.ds(s * shard, step * shard)
         weight1[:, at], peak1[:, at] = weigh(f2[...], f1[at, :], rate)
     for s in range(high):
         if s:
             v2c[s].wait_recv()
         under2[:, span(s)] = values_under(block_two(s), v2[span(s), :], shard, total)
-    for s in reversed(range(0, plane * cores, step)):
+    order = sorted(range(0, plane * cores, step), key=lambda s: (-(s % plane), s))
+    for s in order:
         at = pl.ds(s * shard, step * shard)
         accs, statss = collect(under2[...], weight1[:, at], peak1[:, at], width)
         for n in range(step):
@@ -214,18 +226,19 @@
             if slot:
                 owner = in_plane(-(slot % plane), slot // plane)
                 code1[slot], stat1[slot] = encode(acc, stats)
-                c1c.append(
-                    send(code1.at[slot], got_code1.at[slot], c1s.at[slot], c1r.at[slot], owner)
-                )
-                c1c.append(
-                    send(stat1.at[slot], got_stat1.at[slot], t1s.at[slot], t1r.at[slot], owner)
+                c1c[slot] = (
+                    send(code1.at[slot], got_code1.at[slot], c1s.at[slot], c1r.at[slot], owner),
+                    send(stat1.at[slot], got_stat1.at[slot], t1s.at[slot], t1r.at[slot], owner),
                 )
             else:
                 own1[:width], own1[width:] = acc, stats
 
-    def finish(own, codes, stats, count, block, out):
+    def finish(own, copies, codes, stats, block, out):
         packets = [(own[:width], own[width:])]
-        packets += [(decode(codes[n], stats[n]), stats[n]) for n in range(1, count)]
+        for slot, pair in copies.items():
+            for copy in pair:
+                copy.wait_recv()
+            packets.append((decode(codes[slot], stats[slot]), stats[slot]))
         acc, sums = merge(packets, rate)
         inverse = 1.0 / sums[0:1]
         out[:width] = acc * inverse
@@ -233,12 +246,8 @@
         line = lax.broadcasted_iota(jnp.int32, sums.shape, 0)
         out[width:] = sums * inverse - jnp.where(line == 1, across, down)
 
-    for copy in c2c:
-        copy.wait_recv()
-    finish(own2, got_code2, got_stat2, high, block_two(0), out_two)
-    for copy in c1c:
-        copy.wait_recv()
-    finish(own1, got_code1, got_stat1, plane * cores, block_one(0), out_one)
+    finish(own2, c2c, got_code2, got_stat2, block_two(0), out_two)
+    finish(own1, c1c, got_code1, got_stat1, block_one(0), out_one)
     for copy in started:
         copy.wait_send()
 
@@ -265,7 +274,7 @@
     dma = pltpu.SemaphoreType.DMA
     one, two = pl.pallas_call(
         functools.partial(kernel, dims, total, rate),
-        out_shape=(jax.ShapeDtypeStruct(packet, f32),) * 2,
+        out_shape=(pltpu.VMEM(packet, f32),) * 2,
         in_specs=[pl.BlockSpec(memory_space=pltpu.HBM)] * 4,
         out_specs=[pl.BlockSpec(memory_space=pltpu.VMEM)] * 2,
         scratch_shapes=[
@@ -277,6 +286,8 @@
             vmem((width + EXTRA, n2), bf16),
             vmem((n2, n1), bf16),
             vmem((1, n1), f32),
+            vmem((n1, n2), bf16),
+            vmem((1, n2), f32),
             vmem(packet, f32),
             vmem(packet, f32),
             vmem((plane * cores, width, shard), bf16),
@@ -308,6 +319,7 @@
         ),
         in_specs=[pl.BlockSpec(memory_space=pltpu.VMEM)] * 2,
         out_specs=[pl.BlockSpec(memory_space=pltpu.VMEM)] * 4,
+        compiler_params=pltpu.CompilerParams(vmem_limit_bytes=8 << 20),
         name="place",
     )(one, two)
 

time: 24.5 us -> 21.9 us (0.89)
  Pallas kernels: 23.6 us -> 21.1 us
    pallas_call x1, Pallas kernels: 22 us -> 20.3 us  [body(): pl.pallas_call(functools.partial(kernel, dims, total, rate), out_shape=(p...]
    pallas_call x1, Pallas kernels: 1.67 us -> 0.76 us  [body(): pl.pallas_call(place, out_shape=(jax.ShapeDtypeStruct((shard, width), f32...]
where the time goes in v3:
time: 21.9 us; the launch traced here: 21.7 us
  Pallas kernels  21.1 us (96%)
  between operations  0.64 us (3%)
    pallas_call x1, Pallas kernels, body(): pl.pallas_call(functools.partial(kernel, dims, total, rate), out_shape=(p...  20.3 us
    pallas_call x1, Pallas kernels, body(): pl.pallas_call(place, out_shape=(jax.ShapeDtypeStruct((shard, width), f32...  0.76 us

profile of v3, /device:TPU:0, one launch (start us, length us, event | category | flops | bytes accessed | tf_op | source)
XLA Modules:
  0.0 21.7 jit_solution(18079866125739608585)
XLA Ops:
  0.6 20.3 %match.1 = (f32[136,128]{1,0:T(8,128)S(1)}, f32[136,128]{1,0:T(8,128)S(1)}) custom-call(bf16[128,128]{1,0:T(8,128)(2,1)} %feat_one.1, bf16[128,128]{1,0:T(8,128)(2,1)} %feat_two.1, bf16[128,128]{1,0:T(8,128)(2,1)} %value_one.1, bf16[128,128]{1,0:T(8,128)(2,1)} %value_two.1), custom_call_target="tpu_custom_call" | custom-call | tf_op jit(solution)/shard_map/match/pallas_call | solution.py:275
  21.0 0.8 %place.1 = (f32[128,128]{1,0:T(8,128)}, f32[2,128]{1,0:T(2,128)}, f32[128,128]{1,0:T(8,128)}, f32[2,128]{1,0:T(2,128)}) custom-call(f32[136,128]{1,0:T(8,128)S(1)} %get-tuple-element.6.one, f32[136,128]{1,0:T(8,128)S(1)} %get-tuple-element.7.two), custom_call_target="tpu_custom_call" | custom-call | tf_op jit(solution)/shard_map/place/pallas_call | solution.py:312

commit v4 on v3

--- a/solution.py
+++ b/solution.py
@@ -191,6 +191,9 @@
         if s % wide == wide - 1:
             at = pl.ds((s - wide + 1) * shard, wide * shard)
             weight2[:, at], peak2[:, at] = weigh(f1[...], f2[at, :], rate)
+    for s in reversed(range(0, plane * cores, step)):
+        at = pl.ds(s * shard, step * shard)
+        weight1[:, at], peak1[:, at] = weigh(f2[...], f1[at, :], rate)
     for s, copy in enumerate(v1f):
         copy.wait_recv()
         keep_one(plane + s)
@@ -209,9 +212,6 @@
                 )
             else:
                 own2[:width], own2[width:] = acc, stats
-    for s in reversed(range(0, plane * cores, step)):
-        at = pl.ds(s * shard, step * shard)
-        weight1[:, at], peak1[:, at] = weigh(f2[...], f1[at, :], rate)
     for s in range(high):
         if s:
             v2c[s].wait_recv()

time: 21.9 us -> 21.7 us (level)
  no operation moved by 1% of the time
where the time goes in v4:
time: 21.7 us; the launch traced here: 21.5 us
  Pallas kernels  20.9 us (96%)
  between operations  0.64 us (3%)
    pallas_call x1, Pallas kernels, body(): pl.pallas_call(functools.partial(kernel, dims, total, rate), out_shape=(p...  20.1 us
    pallas_call x1, Pallas kernels, body(): pl.pallas_call(place, out_shape=(jax.ShapeDtypeStruct((shard, width), f32...  0.76 us

profile of v4, /device:TPU:0, one launch (start us, length us, event | category | flops | bytes accessed | tf_op | source)
XLA Modules:
  0.0 21.5 jit_solution(11695752426139159653)
XLA Ops:
  0.6 20.1 %match.1 = (f32[136,128]{1,0:T(8,128)S(1)}, f32[136,128]{1,0:T(8,128)S(1)}) custom-call(bf16[128,128]{1,0:T(8,128)(2,1)} %feat_one.1, bf16[128,128]{1,0:T(8,128)(2,1)} %feat_two.1, bf16[128,128]{1,0:T(8,128)(2,1)} %value_one.1, bf16[128,128]{1,0:T(8,128)(2,1)} %value_two.1), custom_call_target="tpu_custom_call" | custom-call | tf_op jit(solution)/shard_map/match/pallas_call | solution.py:275
  20.8 0.8 %place.1 = (f32[128,128]{1,0:T(8,128)}, f32[2,128]{1,0:T(2,128)}, f32[128,128]{1,0:T(8,128)}, f32[2,128]{1,0:T(2,128)}) custom-call(f32[136,128]{1,0:T(8,128)S(1)} %get-tuple-element.6.one, f32[136,128]{1,0:T(8,128)S(1)} %get-tuple-element.7.two), custom_call_target="tpu_custom_call" | custom-call | tf_op jit(solution)/shard_map/place/pallas_call | solution.py:312
